TPU v7x, 32 devices: a whole 2x2x4 slice. The times are simulated.
32 devices in a mesh: expert: 16 (over z, y, x), dp: 2 (over core).
Axes of the slice: x: 2, y: 2, z: 4, core: 2. Of those that a mesh axis runs over, the one named last changes fastest.
Arguments:
- tokens: bfloat16 [8192, 4096], P('expert', 'dp'), may hold values from -6 to 6
- cotangent: bfloat16 [8192, 4096], P('expert', 'dp'), may hold values from -6 to 6
- routes: int32 [8192, 8], P('expert'), may hold values from 0 to 15, all different within a row; in each aligned block of 512 rows (0 to 511, 512 to 1023, ...) at most 512 rows name the same one
- probs: bfloat16 [8192, 8], P('expert'), may hold values from 0.099609375 to 1
- expert_slot: int32 [16], replicated, may hold values from 0 to 15, each once
- pull_flags: int32 [16], replicated, may hold values 0 or 1
- w_gate: bfloat16 [16, 768, 4096], P('expert', None, 'dp'), may hold values from -0.09375 to 0.09375
- w_up: bfloat16 [16, 768, 4096], P('expert', None, 'dp'), may hold values from -0.09375 to 0.09375
- w_down: bfloat16 [16, 768, 4096], P('expert', None, 'dp'), may hold values from -0.21875 to 0.21875
Outputs:
- expert_out: bfloat16 [8192, 4096], P('expert', 'dp')
- token_grad: bfloat16 [8192, 4096], P('expert', 'dp')
- gate_grad: bfloat16 [16, 768, 4096], P('expert', None, 'dp')
- up_grad: bfloat16 [16, 768, 4096], P('expert', None, 'dp')
- down_grad: bfloat16 [16, 768, 4096], P('expert', None, 'dp')
Inputs may be any that keep to these rules, and one draw needn't show every extreme that they name: `routes`: each row names 8 different experts. Within the 512 rows of one token batch no expert is named by more than 512 rows, and in some batch some expert is named by exactly 512 rows. `expert_slot`: A permutation of the experts.
All inputs are finite; a program needn't handle non-finite values.
Results may differ from a plain program's by a relative error of at most 0.006.
Values may be sent and summed in bfloat16 or wider, within the bound.
No kernel may reach another device: no remote copies, remote signals or barrier semaphores. Data moves between devices by JAX's collectives and lax.ppermute only.
A program may use at most 128 MiB of HBM per device.

v0:
```python
import jax
import jax.numpy as jnp
from jax import lax
from jax.sharding import PartitionSpec as P


def passed_along(value, axis, steps):
    count = lax.axis_size(axis)
    pairs = [(source, (source + steps) % count) for source in range(count)]
    return lax.ppermute(value, axis, pairs)


def silu_parts(gate_val):
    sigmoid_val = jax.nn.sigmoid(gate_val)
    return (gate_val * sigmoid_val, sigmoid_val * (1.0 + gate_val * (1.0 - sigmoid_val)))


def slot_rows(route_ids, weights_in, expert, scale, capacity):
    count = route_ids.shape[0]
    hit = route_ids == expert
    member = jnp.any(hit, axis=1)
    weight = jnp.sum(jnp.where(hit, weights_in.astype(jnp.float32), 0.0), axis=1) * scale
    rank = jnp.cumsum(member.astype(jnp.int32), dtype=jnp.int32) - 1
    entries = jnp.arange(capacity, dtype=jnp.int32)
    chosen = member[None, :] & (rank[None, :] == entries[:, None])
    positions = jnp.arange(count, dtype=jnp.int32)
    index = jnp.sum(jnp.where(chosen, positions[None, :], 0), axis=1, dtype=jnp.int32)
    index = jnp.where(jnp.any(chosen, axis=1), index, count)
    return (index, jnp.take(weight, index, mode="fill", fill_value=0.0))


def hidden_values(gate_val, up_val, back_val, rows_w):
    activated, slope_val = silu_parts(gate_val)
    weight_col = rows_w[..., None]
    scaled = (weight_col * activated * up_val).astype(jnp.bfloat16)
    grad_gate = (back_val * weight_col * up_val * slope_val).astype(jnp.bfloat16)
    grad_up = (back_val * weight_col * activated).astype(jnp.bfloat16)
    return (scaled, grad_gate, grad_up)


def take_rows(array, index):
    return jnp.take(array, index, axis=0, mode="fill", fill_value=0)


def finish_set(scaled, grad_gate, grad_up, rows_x, rows_dy, wg, wu, wd):
    out_rows = jnp.dot(scaled, wd, preferred_element_type=jnp.float32)
    in_rows = jnp.dot(grad_gate, wg, preferred_element_type=jnp.float32)
    in_rows = in_rows + jnp.dot(grad_up, wu, preferred_element_type=jnp.float32)
    over_rows = (((0,), (0,)), ((), ()))
    grad_terms = (
        lax.dot_general(grad_gate, rows_x, over_rows, preferred_element_type=jnp.float32),
        lax.dot_general(grad_up, rows_x, over_rows, preferred_element_type=jnp.float32),
        lax.dot_general(scaled, rows_dy, over_rows, preferred_element_type=jnp.float32),
    )
    return (out_rows, in_rows, tuple((term.astype(jnp.bfloat16) for term in grad_terms)))


def per_device(tokens, cotangent, routes, probs, expert_slot, pull_flags, w_gate, w_up, w_down):
    columns = lax.axis_size("expert")
    column = lax.axis_index("expert")
    count = tokens.shape[0]
    capacity = min(count, count * routes.shape[1] * 2 // columns)
    labels = jnp.arange(columns, dtype=jnp.int32)
    following = (column + 1) % columns

    def owner_expert(slot):
        return jnp.sum(jnp.where(expert_slot == slot, labels, 0), dtype=jnp.int32)

    flag = pull_flags[column].astype(jnp.float32)
    own_index, own_weight = slot_rows(routes, probs, owner_expert(column), 1.0, capacity)
    next_index, next_weight = slot_rows(routes, probs, owner_expert(following), flag, capacity)
    own_x = take_rows(tokens, own_index)
    own_dy = take_rows(cotangent, own_index)
    next_x = take_rows(tokens, next_index)
    next_dy = take_rows(cotangent, next_index)
    own_set = (own_x, own_dy, own_weight, w_gate[0], w_up[0], w_down[0])
    arrived = passed_along((next_x, next_dy, next_weight.astype(jnp.bfloat16)), "expert", 1)
    far_set = (
        arrived[0],
        arrived[1],
        arrived[2].astype(jnp.float32),
        w_gate[0],
        w_up[0],
        w_down[0],
    )
    both_sets = (own_set, far_set)
    contract = (((1,), (1,)), ((), ()))
    partial_gate = jnp.stack(
        [
            lax.dot_general(one[0], one[3], contract, preferred_element_type=jnp.float32)
            for one in both_sets
        ]
    )
    partial_up = jnp.stack(
        [
            lax.dot_general(one[0], one[4], contract, preferred_element_type=jnp.float32)
            for one in both_sets
        ]
    )
    partial_back = jnp.stack(
        [
            lax.dot_general(one[1], one[5], contract, preferred_element_type=jnp.float32)
            for one in both_sets
        ]
    )
    gate_val, up_val, back_val = (
        lax.psum_scatter(partial_gate, "dp", scatter_dimension=2, tiled=True),
        lax.psum_scatter(partial_up, "dp", scatter_dimension=2, tiled=True),
        lax.psum_scatter(partial_back, "dp", scatter_dimension=2, tiled=True),
    )
    rows_w = jnp.stack([own_set[2], far_set[2]])
    scaled, grad_gate, grad_up = hidden_values(gate_val, up_val, back_val, rows_w)
    scaled, grad_gate, grad_up = (
        lax.all_gather(scaled, "dp", axis=2, tiled=True),
        lax.all_gather(grad_gate, "dp", axis=2, tiled=True),
        lax.all_gather(grad_up, "dp", axis=2, tiled=True),
    )
    own_out, own_in, own_grads = finish_set(
        scaled[0],
        grad_gate[0],
        grad_up[0],
        own_set[0],
        own_set[1],
        own_set[3],
        own_set[4],
        own_set[5],
    )
    far_out, far_in, far_grads = finish_set(
        scaled[1],
        grad_gate[1],
        grad_up[1],
        far_set[0],
        far_set[1],
        far_set[3],
        far_set[4],
        far_set[5],
    )
    next_out, next_in = (
        passed_along(far_out.astype(jnp.bfloat16), "expert", -1).astype(far_out.dtype),
        passed_along(far_in.astype(jnp.bfloat16), "expert", -1).astype(far_in.dtype),
    )
    grad_sums = tuple(
        (
            (
                lax.optimization_barrier(mine).astype(jnp.float32)
                + lax.optimization_barrier(theirs).astype(jnp.float32)
            ).astype(jnp.bfloat16)
            for mine, theirs in zip(own_grads, far_grads)
        )
    )
    empty = jnp.zeros(tokens.shape, jnp.float32)
    out_part = (
        empty.at[own_index].add(own_out, mode="drop").at[next_index].add(next_out, mode="drop")
    )
    in_part = empty.at[own_index].add(own_in, mode="drop").at[next_index].add(next_in, mode="drop")
    return (
        out_part.astype(jnp.bfloat16),
        in_part.astype(jnp.bfloat16),
        grad_sums[0][None],
        grad_sums[1][None],
        grad_sums[2][None],
    )


def solution(mesh):
    return jax.shard_map(
        per_device,
        mesh=mesh,
        in_specs=(
            P("expert", "dp"),
            P("expert", "dp"),
            P("expert", None),
            P("expert", None),
            P(),
            P(),
            P("expert", None, "dp"),
            P("expert", None, "dp"),
            P("expert", None, "dp"),
        ),
        out_specs=(
            P("expert", "dp"),
            P("expert", "dp"),
            P("expert", None, "dp"),
            P("expert", None, "dp"),
            P("expert", None, "dp"),
        ),
        check_vma=False,
    )
```

profile of v0, /device:TPU:0, one launch (start us, length us, event | category | flops | bytes accessed | tf_op | source)
XLA Modules:
  0.0 333.3 jit_solution(14110842430651859816)
XLA Ops:
  11.9 7.1 %gather_fusion.5 = bf16[512,2048]{1,0:T(8,128)(2,1)} fusion(bf16[512,2048]{1,0:T(8,128)(2,1)} %param.14, s32[1024]{0:T(1024)S(1)} %pad_clamp_fusion), kind=kCustom, calls=%fused_computation.5.clone | custom fusion | bytes 4196352 | tf_op jit(solution)/shard_map/jit(_take)/gather | solution.py:42
  19.0 7.1 %gather_fusion.3 = bf16[512,2048]{1,0:T(8,128)(2,1)} fusion(bf16[512,2048]{1,0:T(8,128)(2,1)} %param.13, s32[1024]{0:T(1024)S(1)} %pad_clamp_fusion), kind=kCustom, calls=%fused_computation.3.clone | custom fusion | bytes 4196352 | tf_op jit(solution)/shard_map/jit(_take)/gather | solution.py:42
  30.9 4.6 %broadcast_select_fusion = (bf16[512,2048]{1,0:T(8,128)(2,1)}, bf16[512,2048]{1,0:T(8,128)(2,1)}) fusion(bf16[512,2048]{1,0:T(8,128)(2,1)} %gather_fusion.5, pred[512]{0:T(512)(128)(4,1)S(1)} %get-tuple-element.14, bf16[512,2048]{1,0:T(8,128)(2,1)} %gather_fusion.3), kind=kLoop, calls=%fused_computation.60 | loop fusion | flops 2097152 | bytes 8389120 | tf_op jit(solution)/shard_map/jit(_take)/select_n | solution.py:42
  40.1 7.1 %gather_fusion.2 = bf16[512,2048]{1,0:T(8,128)(2,1)} fusion(bf16[512,2048]{1,0:T(8,128)(2,1)} %param.13, s32[1024]{0:T(1024)S(1)} %pad_clamp_fusion.1), kind=kCustom, calls=%fused_computation.1.clone | custom fusion | bytes 4196352 | tf_op jit(solution)/shard_map/jit(_take)/gather | solution.py:42
  50.8 4.5 %fusion.42 = f32[1,512,768]{2,1,0:T(8,128)S(1)} fusion(bf16[1,768,2048]{2,1,0:T(8,128)(2,1)} %param.19, bf16[512,2048]{1,0:T(8,128)(2,1)} %gather_fusion.2, pred[512]{0:T(512)(128)(4,1)S(1)} %get-tuple-element.12), kind=kOutput, calls=%fused_computation.69 | convolution fusion | flops 1611661312 | bytes 6816256 | tf_op jit(solution)/shard_map/dot_general | solution.py:90
  55.3 33.6 %collective-permute-done.1 = bf16[512,2048]{1,0:T(8,128)(2,1)} collective-permute-done((bf16[512,2048]{1,0:T(8,128)(2,1)}, bf16[512,2048]{1,0:T(8,128)(2,1)}, u32[]{:S(2)}, u32[]{:S(2)}) %collective-permute-start.1) | collective-permute-done | bytes 2097184 | tf_op jit(solution)/shard_map/ppermute | solution.py:10
  103.5 7.1 %gather_fusion.4 = bf16[512,2048]{1,0:T(8,128)(2,1)} fusion(bf16[512,2048]{1,0:T(8,128)(2,1)} %param.14, s32[1024]{0:T(1024)S(1)} %pad_clamp_fusion.1), kind=kCustom, calls=%fused_computation.4.clone | custom fusion | bytes 4196352 | tf_op jit(solution)/shard_map/jit(_take)/gather | solution.py:42
  110.6 4.9 %fusion.54 = f32[1,512,768]{2,1,0:T(8,128)S(1)} fusion(bf16[1,768,2048]{2,1,0:T(8,128)(2,1)} %param.21, bf16[512,2048]{1,0:T(8,128)(2,1)} %gather_fusion.4, pred[512]{0:T(512)(128)(4,1)S(1)} %get-tuple-element.12), kind=kOutput, calls=%fused_computation.73 | convolution fusion | flops 1611661312 | bytes 6816256 | tf_op jit(solution)/shard_map/dot_general | solution.py:102
  115.5 39.0 %collective-permute-done.3 = bf16[512,2048]{1,0:T(8,128)(2,1)} collective-permute-done((bf16[512,2048]{1,0:T(8,128)(2,1)}, bf16[512,2048]{1,0:T(8,128)(2,1)}, u32[]{:S(2)}, u32[]{:S(2)}) %collective-permute-start.3) | collective-permute-done | bytes 2097184 | tf_op jit(solution)/shard_map/ppermute | solution.py:10
  159.9 7.2 %collective-permute-done = bf16[512]{0:T(512)(128)(2,1)S(1)} collective-permute-done((bf16[512]{0:T(512)(128)(2,1)S(1)}, bf16[512]{0:T(512)(128)(2,1)S(1)}, u32[]{:S(2)}, u32[]{:S(2)}) %collective-permute-start) | collective-permute-done | bytes 1056 | tf_op jit(solution)/shard_map/ppermute | solution.py:10
  167.2 4.7 %multiply_convert_fusion = (bf16[2,512,384]{2,1,0:T(8,128)(2,1)}, bf16[2,512,384]{2,1,0:T(8,128)(2,1)}, bf16[2,512,384]{2,1,0:T(8,128)(2,1)}) fusion(f32[2,512,384]{2,1,0:T(8,128)} %reduce-scatter.8.cloned.1.call-done, f32[2,512]{1,0:T(2,128)S(1)} %pad_maximum_fusion.3, f32[2,512,384]{2,1,0:T(8,128)} %reduce-scatter.4.cloned.1.call-done, ...), kind=kLoop, calls=%fused_computation.64 | loop fusion | flops 6684672 | bytes 7081984 | tf_op jit(solution)/shard_map/convert_element_type | solution.py:37
  173.1 9.6 %all-gather.8.cloned.1.call-done = bf16[2,512,768]{2,1,0:T(8,128)(2,1)} async-done(((bf16[2,512,384]{2,1,0:T(8,128)(2,1)}), bf16[2,512,768]{2,1,0:T(8,128)(2,1)}) %all-gather.8.cloned.1.call-update) | async-done | bytes 1572880 | tf_op jit(solution)/shard_map/all_gather | solution.py:116
  182.7 4.9 %fusion.17 = f32[512,2048]{1,0:T(8,128)} fusion(bf16[1,768,2048]{2,1,0:T(8,128)(2,1)S(1)} %copy-done, bf16[2,512,768]{2,1,0:T(8,128)(2,1)} %all-gather.8.cloned.1.call-done), kind=kOutput, calls=%fused_computation.40 | convolution fusion | flops 1610612736 | bytes 8126464 | tf_op jit(solution)/shard_map/dot_general | solution.py:48
  187.5 8.1 %all-gather.6.cloned.1.call-done = bf16[2,512,768]{2,1,0:T(8,128)(2,1)} async-done(((bf16[2,512,384]{2,1,0:T(8,128)(2,1)}), bf16[2,512,768]{2,1,0:T(8,128)(2,1)}) %all-gather.6.cloned.1.call-update) | async-done | bytes 1572880 | tf_op jit(solution)/shard_map/all_gather | solution.py:115
  195.6 6.5 %add_convert_fusion.3 = bf16[512,2048]{1,0:T(8,128)(2,1)} fusion(f32[512,2048]{1,0:T(8,128)} %fusion.17, bf16[1,768,2048]{2,1,0:T(8,128)(2,1)} %param.19, bf16[2,512,768]{2,1,0:T(8,128)(2,1)} %all-gather.6.cloned.1.call-done), kind=kOutput, calls=%fused_computation.15 | convolution fusion | flops 1612709888 | bytes 10223616 | tf_op jit(solution)/shard_map/dot_general | solution.py:47
  202.1 5.4 %collective-permute-start.4 = (bf16[512,2048]{1,0:T(8,128)(2,1)}, bf16[512,2048]{1,0:T(8,128)(2,1)}, u32[]{:S(2)}, u32[]{:S(2)}) collective-permute-start(bf16[512,2048]{1,0:T(8,128)(2,1)} %add_convert_fusion.3), channel_id=1, source_target_pairs={{0,30},{2,0},{4,2},{6,4},{8,6},{10,8},{12,10},{14,12},{16,14},{18,... | collective-permute-start | bytes 6291464 | tf_op jit(solution)/shard_map/ppermute | solution.py:10
  208.5 5.3 %fusion.33 = bf16[512,2048]{1,0:T(8,128)(2,1)} fusion(bf16[1,768,2048]{2,1,0:T(8,128)(2,1)} %param.21, bf16[2,512,768]{2,1,0:T(8,128)(2,1)} %all-gather.4.cloned.1.call-done), kind=kOutput, calls=%fused_computation.56 | convolution fusion | flops 1611661312 | bytes 6029312 | tf_op jit(solution)/shard_map/dot_general | solution.py:46
  213.9 5.6 %collective-permute-start.2 = (bf16[512,2048]{1,0:T(8,128)(2,1)}, bf16[512,2048]{1,0:T(8,128)(2,1)}, u32[]{:S(2)}, u32[]{:S(2)}) collective-permute-start(bf16[512,2048]{1,0:T(8,128)(2,1)} %fusion.33), channel_id=1, source_target_pairs={{0,30},{2,0},{4,2},{6,4},{8,6},{10,8},{12,10},{14,12},{16,14},{18,... | collective-permute-start | bytes 6291464 | tf_op jit(solution)/shard_map/ppermute | solution.py:10
  219.5 5.1 %convolution_convert_fusion.2 = bf16[768,2048]{1,0:T(8,128)(2,1)} fusion(bf16[512,2048]{1,0:T(8,128)(2,1)} %collective-permute-done.1, bf16[2,512,768]{2,1,0:T(8,128)(2,1)S(1)} %copy-done.11), kind=kOutput, calls=%fused_computation.22 | convolution fusion | flops 1612185600 | bytes 6029312 | tf_op jit(solution)/shard_map/dot_general | solution.py:52
  228.1 5.2 %convolution_convert_fusion = bf16[768,2048]{1,0:T(8,128)(2,1)} fusion(bf16[512,2048]{1,0:T(8,128)(2,1)} %collective-permute-done.3, bf16[2,512,768]{2,1,0:T(8,128)(2,1)S(1)} %copy-done.13), kind=kOutput, calls=%fused_computation.20 | convolution fusion | flops 1612185600 | bytes 6029312 | tf_op jit(solution)/shard_map/dot_general | solution.py:53
  233.4 3.6 %convolution_convert_fusion.1 = bf16[768,2048]{1,0:T(8,128)(2,1)} fusion(bf16[512,2048]{1,0:T(8,128)(2,1)S(1)} %copy-done.6, pred[512]{0:T(512)(128)(4,1)S(1)} %get-tuple-element.12, bf16[2,512,768]{2,1,0:T(8,128)(2,1)S(1)} %copy-done.13), kind=kOutput, calls=%fused_computation.21 | convolution fusion | flops 1613234176 | bytes 6029824 | tf_op jit(solution)/shard_map/dot_general | solution.py:53
  240.6 3.8 %fusion.19 = f32[512,2048]{1,0:T(8,128)} fusion(bf16[1,768,2048]{2,1,0:T(8,128)(2,1)S(1)} %copy-done, bf16[2,512,768]{2,1,0:T(8,128)(2,1)S(1)} %copy-done.11), kind=kOutput, calls=%fused_computation.42 | convolution fusion | flops 1610612736 | bytes 8126464 | tf_op jit(solution)/shard_map/dot_general | solution.py:48
  244.4 3.8 %fusion.27 = f32[512,2048]{1,0:T(8,128)} fusion(bf16[1,768,2048]{2,1,0:T(8,128)(2,1)S(1)} %copy-done.8, bf16[2,512,768]{2,1,0:T(8,128)(2,1)S(1)} %copy-done.12), kind=kOutput, calls=%fused_computation.50 | convolution fusion | flops 1610612736 | bytes 8126464 | tf_op jit(solution)/shard_map/dot_general | solution.py:47
  248.2 3.8 %fusion.15 = f32[512,2048]{1,0:T(8,128)} fusion(bf16[1,768,2048]{2,1,0:T(8,128)(2,1)S(1)} %copy-done.10, bf16[2,512,768]{2,1,0:T(8,128)(2,1)S(1)} %copy-done.13), kind=kOutput, calls=%fused_computation.38 | convolution fusion | flops 1610612736 | bytes 8126464 | tf_op jit(solution)/shard_map/dot_general | solution.py:46
  251.9 5.5 %convolution_convert_fusion.4 = bf16[768,2048]{1,0:T(8,128)(2,1)} fusion(bf16[512,2048]{1,0:T(8,128)(2,1)} %collective-permute-done.1, bf16[2,512,768]{2,1,0:T(8,128)(2,1)S(1)} %copy-done.12), kind=kOutput, calls=%fused_computation.24 | convolution fusion | flops 1612185600 | bytes 6029312 | tf_op jit(solution)/shard_map/dot_general | solution.py:51
  257.5 10.7 %scatter_custom_fusion = f32[512,2048]{1,0:T(8,128)} fusion(s32[512]{0:T(512)S(1)} %bitcast.112, f32[512,2048]{1,0:T(8,128)} %fusion.15, f32[]{:T(128)} %constant.31.clone.1), kind=kCustom, calls=%fused_computation.58 | custom fusion | flops 1048576 | bytes 4194816 | tf_op jit(solution)/shard_map/scatter-add | solution.py:153
  268.2 12.5 %scatter_custom_fusion.2 = f32[512,2048]{1,0:T(8,128)} fusion(s32[512]{0:T(512)S(1)} %bitcast.113, f32[512,2048]{1,0:T(8,128)} %fusion.27, f32[512,2048]{1,0:T(8,128)} %fusion.19, f32[]{:T(128)} %constant.31.clone.1), kind=kCustom, calls=%fused_computation.16 | custom fusion | flops 2097152 | bytes 12582916 | tf_op jit(solution)/shard_map/scatter-add | solution.py:155
  280.8 6.2 %fusion.7 = bf16[1,768,2048]{2,1,0:T(8,128)(2,1)} fusion(bf16[768,2048]{1,0:T(8,128)(2,1)} %convolution_convert_fusion.2, bf16[768,2048]{1,0:T(8,128)(2,1)} %convolution_convert_fusion.3), kind=kLoop, calls=%fused_computation.27 | loop fusion | flops 6291456 | bytes 9437184 | tf_op jit(solution)/shard_map/broadcast_in_dim | solution.py:160
  293.9 12.4 %scatter_custom_fusion.3 = f32[512,2048]{1,0:T(8,128)} fusion(f32[512,2048]{1,0:T(8,128)} %scatter_custom_fusion.2, s32[512]{0:T(512)S(1)} %bitcast.110, bf16[512,2048]{1,0:T(8,128)(2,1)} %collective-permute-done.4), kind=kCustom, calls=%fused_computation.13 | custom fusion | flops 2097152 | bytes 6291456 | tf_op jit(solution)/shard_map/scatter-add | solution.py:155
  306.4 3.8 %convert_element_type.116 = bf16[512,2048]{1,0:T(8,128)(2,1)} convert(f32[512,2048]{1,0:T(8,128)} %scatter_custom_fusion.3) | non-fusion elementwise | flops 1048576 | bytes 6291456 | tf_op jit(solution)/shard_map/convert_element_type | solution.py:158
  310.2 12.2 %scatter_custom_fusion.1 = f32[512,2048]{1,0:T(8,128)} fusion(f32[512,2048]{1,0:T(8,128)} %scatter_custom_fusion, s32[512]{0:T(512)S(1)} %bitcast.111, bf16[512,2048]{1,0:T(8,128)(2,1)} %collective-permute-done.2), kind=kCustom, calls=%fused_computation.18 | custom fusion | flops 2097152 | bytes 6291456 | tf_op jit(solution)/shard_map/scatter-add | solution.py:153
  322.4 3.8 %convert_element_type.111 = bf16[512,2048]{1,0:T(8,128)(2,1)} convert(f32[512,2048]{1,0:T(8,128)} %scatter_custom_fusion.1) | non-fusion elementwise | flops 1048576 | bytes 6291456 | tf_op jit(solution)/shard_map/convert_element_type | solution.py:157
  (96 shorter events, 53.2 us)
Async XLA Ops:
  7.2 87.1 %copy-start = (bf16[1,768,2048]{2,1,0:T(8,128)(2,1)S(1)}, bf16[1,768,2048]{2,1,0:T(8,128)(2,1)}, u32[]{:S(2)}) copy-start(bf16[1,768,2048]{2,1,0:T(8,128)(2,1)} %param.20) | copy-start | bytes 9437188
  7.2 159.9 %reduce-scatter.4.cloned.1.call-start = ((), (), s32[]{:S(2)}) async-start(), calls=%async_computation.3 | async-start | bytes 4718592 | tf_op jit(solution)/shard_map/reduce_scatter | solution.py:107
  19.0 7.1 %copy-start.14 = (s32[16]{0:T(128)S(1)}, s32[16]{0:T(128)}, u32[]{:S(2)}) copy-start(s32[16]{0:T(128)} %param.18) | copy-start | bytes 196
  35.5 53.4 %collective-permute-start.1 = (bf16[512,2048]{1,0:T(8,128)(2,1)}, bf16[512,2048]{1,0:T(8,128)(2,1)}, u32[]{:S(2)}, u32[]{:S(2)}) collective-permute-start(bf16[512,2048]{1,0:T(8,128)(2,1)} %get-tuple-element.25), channel_id=1, source_target_pairs={{0,2},{2,4},{4,6},{6,8},{8,10},{10,12},{12,14},{14,16},{16,18},{18... | collective-permute-start | bytes 6291464 | tf_op jit(solution)/shard_map/ppermute | solution.py:10
  50.8 38.1 %copy-start.7 = (bf16[1,768,2048]{2,1,0:T(8,128)(2,1)S(1)}, bf16[1,768,2048]{2,1,0:T(8,128)(2,1)}, u32[]{:S(2)}) copy-start(bf16[1,768,2048]{2,1,0:T(8,128)(2,1)} %param.19) | copy-start | bytes 9437188
  94.2 72.9 %reduce-scatter.6.cloned.1.call-start = ((), (), s32[]{:S(2)}) async-start(), calls=%async_computation.4 | async-start | bytes 4718592 | tf_op jit(solution)/shard_map/reduce_scatter | solution.py:108
  103.2 64.0 %reduce-scatter.8.cloned.1.call-start = ((), (), s32[]{:S(2)}) async-start(), calls=%async_computation.6 | async-start | bytes 4718592 | tf_op jit(solution)/shard_map/reduce_scatter | solution.py:109
  103.3 51.2 %collective-permute-start.3 = (bf16[512,2048]{1,0:T(8,128)(2,1)}, bf16[512,2048]{1,0:T(8,128)(2,1)}, u32[]{:S(2)}, u32[]{:S(2)}) collective-permute-start(bf16[512,2048]{1,0:T(8,128)(2,1)} %get-tuple-element.24), channel_id=1, source_target_pairs={{0,2},{2,4},{4,6},{6,8},{8,10},{10,12},{12,14},{14,16},{16,18},{18... | collective-permute-start | bytes 6291464 | tf_op jit(solution)/shard_map/ppermute | solution.py:10
  110.6 43.9 %copy-start.9 = (bf16[1,768,2048]{2,1,0:T(8,128)(2,1)S(1)}, bf16[1,768,2048]{2,1,0:T(8,128)(2,1)}, u32[]{:S(2)}) copy-start(bf16[1,768,2048]{2,1,0:T(8,128)(2,1)} %param.21) | copy-start | bytes 9437188
  159.8 22.9 %all-gather.8.cloned.1.call-start = ((), (), s32[]{:S(2)}) async-start(), calls=%async_computation.8 | async-start | bytes 2359296 | tf_op jit(solution)/shard_map/all_gather | solution.py:116
  159.9 7.2 %collective-permute-start = (bf16[512]{0:T(512)(128)(2,1)S(1)}, bf16[512]{0:T(512)(128)(2,1)S(1)}, u32[]{:S(2)}, u32[]{:S(2)}) collective-permute-start(bf16[512]{0:T(512)(128)(2,1)S(1)} %get-tuple-element.13), channel_id=1, source_target_pairs={{0,2},{2,4},{4,6},{6,8},{8,10},{10,12},{12,14},{14,16},{16,18},{18... | collective-permute-start | bytes 3080 | tf_op jit(solution)/shard_map/ppermute | solution.py:10
  171.9 23.7 %all-gather.6.cloned.1.call-start = ((), (), s32[]{:S(2)}) async-start(), calls=%async_computation.7 | async-start | bytes 2359296 | tf_op jit(solution)/shard_map/all_gather | solution.py:115
  172.5 36.1 %all-gather.4.cloned.1.call-start = ((), (), s32[]{:S(2)}) async-start(), calls=%async_computation.5 | async-start | bytes 2359296 | tf_op jit(solution)/shard_map/all_gather | solution.py:114
  202.1 91.8 %collective-permute-start.4 = (bf16[512,2048]{1,0:T(8,128)(2,1)}, bf16[512,2048]{1,0:T(8,128)(2,1)}, u32[]{:S(2)}, u32[]{:S(2)}) collective-permute-start(bf16[512,2048]{1,0:T(8,128)(2,1)} %add_convert_fusion.3), channel_id=1, source_target_pairs={{0,30},{2,0},{4,2},{6,4},{8,6},{10,8},{12,10},{14,12},{16,14},{18,... | collective-permute-start | bytes 6291464 | tf_op jit(solution)/shard_map/ppermute | solution.py:10
  208.5 10.9 %copy-start.11 = (bf16[2,512,768]{2,1,0:T(8,128)(2,1)S(1)}, bf16[2,512,768]{2,1,0:T(8,128)(2,1)}, u32[]{:S(2)}) copy-start(bf16[2,512,768]{2,1,0:T(8,128)(2,1)} %all-gather.8.cloned.1.call-done) | copy-start | bytes 4718596
  213.9 10.7 %copy-start.5 = (bf16[512,2048]{1,0:T(8,128)(2,1)S(1)}, bf16[512,2048]{1,0:T(8,128)(2,1)}, u32[]{:S(2)}) copy-start(bf16[512,2048]{1,0:T(8,128)(2,1)} %gather_fusion.2) | copy-start | bytes 6291460
  213.9 96.3 %collective-permute-start.2 = (bf16[512,2048]{1,0:T(8,128)(2,1)}, bf16[512,2048]{1,0:T(8,128)(2,1)}, u32[]{:S(2)}, u32[]{:S(2)}) collective-permute-start(bf16[512,2048]{1,0:T(8,128)(2,1)} %fusion.33), channel_id=1, source_target_pairs={{0,30},{2,0},{4,2},{6,4},{8,6},{10,8},{12,10},{14,12},{16,14},{18,... | collective-permute-start | bytes 6291464 | tf_op jit(solution)/shard_map/ppermute | solution.py:10
  224.6 3.6 %copy-start.13 = (bf16[2,512,768]{2,1,0:T(8,128)(2,1)S(1)}, bf16[2,512,768]{2,1,0:T(8,128)(2,1)}, u32[]{:S(2)}) copy-start(bf16[2,512,768]{2,1,0:T(8,128)(2,1)} %all-gather.4.cloned.1.call-done) | copy-start | bytes 4718596
  228.1 5.2 %copy-start.6 = (bf16[512,2048]{1,0:T(8,128)(2,1)S(1)}, bf16[512,2048]{1,0:T(8,128)(2,1)}, u32[]{:S(2)}) copy-start(bf16[512,2048]{1,0:T(8,128)(2,1)} %gather_fusion.4) | copy-start | bytes 6291460
  233.4 3.6 %copy-start.12 = (bf16[2,512,768]{2,1,0:T(8,128)(2,1)S(1)}, bf16[2,512,768]{2,1,0:T(8,128)(2,1)}, u32[]{:S(2)}) copy-start(bf16[2,512,768]{2,1,0:T(8,128)(2,1)} %all-gather.6.cloned.1.call-done) | copy-start | bytes 4718596
  240.6 3.8 %copy-start.8 = (bf16[1,768,2048]{2,1,0:T(8,128)(2,1)S(1)}, bf16[1,768,2048]{2,1,0:T(8,128)(2,1)}, u32[]{:S(2)}) copy-start(bf16[1,768,2048]{2,1,0:T(8,128)(2,1)} %param.19) | copy-start | bytes 9437188
  244.4 3.8 %copy-start.10 = (bf16[1,768,2048]{2,1,0:T(8,128)(2,1)S(1)}, bf16[1,768,2048]{2,1,0:T(8,128)(2,1)}, u32[]{:S(2)}) copy-start(bf16[1,768,2048]{2,1,0:T(8,128)(2,1)} %param.21) | copy-start | bytes 9437188
  280.7 6.3 %copy-start.1 = (bf16[768,2048]{1,0:T(8,128)(2,1)S(1)}, bf16[768,2048]{1,0:T(8,128)(2,1)}, u32[]{:S(2)}) copy-start(bf16[768,2048]{1,0:T(8,128)(2,1)} %convolution_convert_fusion) | copy-start | bytes 9437188
  280.7 6.3 %copy-start.2 = (bf16[768,2048]{1,0:T(8,128)(2,1)S(1)}, bf16[768,2048]{1,0:T(8,128)(2,1)}, u32[]{:S(2)}) copy-start(bf16[768,2048]{1,0:T(8,128)(2,1)} %convolution_convert_fusion.1) | copy-start | bytes 9437188
  287.0 3.1 copy-start.3
  287.0 3.8 %copy-start.4 = (bf16[768,2048]{1,0:T(8,128)(2,1)S(1)}, bf16[768,2048]{1,0:T(8,128)(2,1)}, u32[]{:S(2)}) copy-start(bf16[768,2048]{1,0:T(8,128)(2,1)} %convolution_convert_fusion.4) | copy-start | bytes 9437188
Sparse Core Ops, SparseCore 0:
  94.3 8.4 reduce-scatter.3
  105.6 12.2 reduce-scatter.5
  159.9 6.8 reduce-scatter.7
  172.0 10.6 all-gather.7
  184.6 10.9 all-gather.5
  197.6 10.9 all-gather.3
where the time goes:
time: 339 us; the launch traced here: 333 us
  waiting for transfers between devices  99.6 us (29%)
  other arithmetic  88.3 us (26%)
  matrix products  78 us (23%)
  local copies, waits for them, and re-layouts  37.1 us (11%)
  between operations  15.3 us (5%)
  starting transfers between devices  15 us (4%)
    ppermute x5, waiting for transfers between devices, passed_along(): return lax.ppermute(value, axis, pairs)  79.7 us
    gather x4, local copies, waits for them, and re-layouts, take_rows(): return jnp.take(array, index, axis=0, mode='fill', fill_value=0)  28.4 us
    scatter-add x2, other arithmetic, per_device(): empty.at[own_index].add(own_in, mode='drop').at[next_index]  25 us
    scatter-add x2, other arithmetic, per_device(): empty.at[own_index].add(own_out, mode='drop').at[next_index]  22.9 us
    ppermute x5, starting transfers between devices, passed_along(): return lax.ppermute(value, axis, pairs)  14.8 us
    dot_general x2, matrix products, finish_set(): in_rows = jnp.dot(grad_gate, wg, preferred_element_type=jnp.float32)  10.3 us
    all_gather x1, waiting for transfers between devices, per_device(): lax.all_gather(grad_up, 'dp', axis=2, tiled=True)  9.61 us
    dot_general x2, matrix products, finish_set(): out_rows = jnp.dot(scaled, wd, preferred_element_type=jnp.float32)  9.12 us
  transfers between devices with their start and end apart: 11, of which 6 were waited for; matrix products, arithmetic and copies ran while one was open for 45% of the time, Pallas kernels for 0%

commit v1 on v0

--- a/solution.py
+++ b/solution.py
@@ -112,7 +112,9 @@
     scaled, grad_gate, grad_up = hidden_values(gate_val, up_val, back_val, rows_w)
     scaled, grad_gate, grad_up = (
         lax.all_gather(scaled, "dp", axis=2, tiled=True),
-        lax.all_gather(grad_gate, "dp", axis=2, tiled=True),
+        jnp.concatenate(
+            lax.all_to_all(jnp.stack([grad_gate] * lax.axis_size("dp")), "dp", 0, 0), axis=2
+        ),
         lax.all_gather(grad_up, "dp", axis=2, tiled=True),
     )
     own_out, own_in, own_grads = finish_set(

time: 339 us -> 349 us (1.029)
  waiting for transfers between devices: 99.6 us -> 108 us
  local copies, waits for them, and re-layouts: 37.1 us -> 42.4 us
  starting transfers between devices: 15 us -> 9.79 us
  blocking collectives: 0 us -> 5 us
  matrix products: 78 us -> 73.2 us
    ppermute x5, waiting for transfers between devices: 79.7 us -> 108 us  [passed_along(): return lax.ppermute(value, axis, pairs)]
    all_gather x1, waiting for transfers between devices: 9.61 us -> 0.01 us  [per_device(): lax.all_gather(grad_up, 'dp', axis=2, tiled=True)]
    all_gather x1 -> x0, waiting for transfers between devices: 8.07 us -> none  [per_device(): lax.all_gather(grad_gate, 'dp', axis=2, tiled=True)]
    slice x1 -> x4, local copies, waits for them, and re-layouts: 0.07 us -> 6.07 us  [the longest x2 3.71 us: per_device(): grad_gate[1]]
    ppermute x5, starting transfers between devices: 14.8 us -> 9.59 us  [passed_along(): return lax.ppermute(value, axis, pairs)]
    all_to_all x0 -> x1, blocking collectives: none -> 5 us  [per_device(): lax.all_to_all(jnp.stack([grad_gate] * lax.axis_size('dp')), 'dp', 0, 0)]
  transfers between devices with their start and end apart: 11 -> 10, of which waited for: 6 -> 5; matrix products, arithmetic and copies ran while one was open for 45% -> 40% of each run, Pallas kernels for 0% -> 0%
where the time goes in v1:
time: 349 us; the launch traced here: 344 us
  waiting for transfers between devices  108 us (31%)
  other arithmetic  90.2 us (26%)
  matrix products  73.2 us (21%)
  local copies, waits for them, and re-layouts  42.4 us (12%)
  between operations  14.9 us (4%)
  starting transfers between devices  9.79 us (3%)
  blocking collectives  5 us (1%)
    ppermute x5, waiting for transfers between devices, passed_along(): return lax.ppermute(value, axis, pairs)  108 us
    gather x4, local copies, waits for them, and re-layouts, take_rows(): return jnp.take(array, index, axis=0, mode='fill', fill_value=0)  28.4 us
    scatter-add x2, other arithmetic, per_device(): empty.at[own_index].add(own_in, mode='drop').at[next_index]  24.9 us
    scatter-add x2, other arithmetic, per_device(): empty.at[own_index].add(own_out, mode='drop').at[next_index]  23.3 us
    ppermute x5, starting transfers between devices, passed_along(): return lax.ppermute(value, axis, pairs)  9.59 us
    dot_general x2, matrix products, finish_set(): lax.dot_general(scaled, rows_dy, over_rows, preferred_element_type=jnp.fl...  9.31 us
    dot_general x2, matrix products, finish_set(): lax.dot_general(grad_up, rows_x, over_rows, preferred_element_type=jnp.fl...  9.29 us
    dot_general x2, matrix products, finish_set(): lax.dot_general(grad_gate, rows_x, over_rows, preferred_element_type=jnp....  9.21 us
  transfers between devices with their start and end apart: 10, of which 5 were waited for; matrix products, arithmetic and copies ran while one was open for 40% of the time, Pallas kernels for 0%

profile of v1, /device:TPU:0, one launch (start us, length us, event | category | flops | bytes accessed | tf_op | source)
XLA Modules:
  0.0 343.7 jit_solution(10943472209555040953)
XLA Ops:
  11.9 7.1 %gather_fusion.5 = bf16[512,2048]{1,0:T(8,128)(2,1)} fusion(bf16[512,2048]{1,0:T(8,128)(2,1)} %param.14, s32[1024]{0:T(1024)S(1)} %pad_clamp_fusion), kind=kCustom, calls=%fused_computation.5.clone | custom fusion | bytes 4196352 | tf_op jit(solution)/shard_map/jit(_take)/gather | solution.py:42
  19.0 7.1 %gather_fusion.3 = bf16[512,2048]{1,0:T(8,128)(2,1)} fusion(bf16[512,2048]{1,0:T(8,128)(2,1)} %param.13, s32[1024]{0:T(1024)S(1)} %pad_clamp_fusion), kind=kCustom, calls=%fused_computation.3.clone | custom fusion | bytes 4196352 | tf_op jit(solution)/shard_map/jit(_take)/gather | solution.py:42
  27.4 3.5 %gather_fusion.1 = bf16[512]{0:T(512)(128)(2,1)S(1)} fusion(bf16[512]{0:T(512)(128)(2,1)S(1)} %broadcast_multiply_fusion, s32[1024]{0:T(1024)S(1)} %pad_clamp_fusion), kind=kCustom, calls=%fused_computation.2.clone | custom fusion | bytes 4096 | tf_op jit(solution)/shard_map/jit(_take)/gather | solution.py:29
  30.9 4.6 %broadcast_select_fusion = (bf16[512,2048]{1,0:T(8,128)(2,1)}, bf16[512,2048]{1,0:T(8,128)(2,1)}) fusion(bf16[512,2048]{1,0:T(8,128)(2,1)} %gather_fusion.5, pred[512]{0:T(512)(128)(4,1)S(1)} %get-tuple-element.14, bf16[512,2048]{1,0:T(8,128)(2,1)} %gather_fusion.3), kind=kLoop, calls=%fused_computation.60 | loop fusion | flops 2097152 | bytes 8389120 | tf_op jit(solution)/shard_map/jit(_take)/select_n | solution.py:42
  39.9 7.1 %gather_fusion.2 = bf16[512,2048]{1,0:T(8,128)(2,1)} fusion(bf16[512,2048]{1,0:T(8,128)(2,1)} %param.13, s32[1024]{0:T(1024)S(1)} %pad_clamp_fusion.1), kind=kCustom, calls=%fused_computation.1.clone | custom fusion | bytes 4196352 | tf_op jit(solution)/shard_map/jit(_take)/gather | solution.py:42
  47.0 3.5 %gather_fusion = f32[512]{0:T(512)S(1)} fusion(f32[512]{0:T(512)S(1)} %get-tuple-element.7, s32[1024]{0:T(1024)S(1)} %pad_clamp_fusion.1), kind=kCustom, calls=%fused_computation.clone | custom fusion | bytes 6144 | tf_op jit(solution)/shard_map/jit(_take)/gather | solution.py:29
  53.9 34.7 %collective-permute-done.1 = bf16[512,2048]{1,0:T(8,128)(2,1)} collective-permute-done((bf16[512,2048]{1,0:T(8,128)(2,1)}, bf16[512,2048]{1,0:T(8,128)(2,1)}, u32[]{:S(2)}, u32[]{:S(2)}) %collective-permute-start.1) | collective-permute-done | bytes 2097184 | tf_op jit(solution)/shard_map/ppermute | solution.py:10
  94.0 4.5 %fusion.48 = f32[1,512,768]{2,1,0:T(8,128)S(1)} fusion(bf16[1,768,2048]{2,1,0:T(8,128)(2,1)} %param.20, bf16[512,2048]{1,0:T(8,128)(2,1)} %gather_fusion.2, pred[512]{0:T(512)(128)(4,1)S(1)} %get-tuple-element.12), kind=kOutput, calls=%fused_computation.72 | convolution fusion | flops 1611661312 | bytes 6816256 | tf_op jit(solution)/shard_map/dot_general | solution.py:96
  104.5 7.1 %gather_fusion.4 = bf16[512,2048]{1,0:T(8,128)(2,1)} fusion(bf16[512,2048]{1,0:T(8,128)(2,1)} %param.14, s32[1024]{0:T(1024)S(1)} %pad_clamp_fusion.1), kind=kCustom, calls=%fused_computation.4.clone | custom fusion | bytes 4196352 | tf_op jit(solution)/shard_map/jit(_take)/gather | solution.py:42
  111.6 5.5 %fusion.54 = f32[1,512,768]{2,1,0:T(8,128)S(1)} fusion(bf16[1,768,2048]{2,1,0:T(8,128)(2,1)} %param.21, bf16[512,2048]{1,0:T(8,128)(2,1)} %gather_fusion.4, pred[512]{0:T(512)(128)(4,1)S(1)} %get-tuple-element.12), kind=kOutput, calls=%fused_computation.74 | convolution fusion | flops 1611661312 | bytes 6816256 | tf_op jit(solution)/shard_map/dot_general | solution.py:102
  117.1 38.3 %collective-permute-done.3 = bf16[512,2048]{1,0:T(8,128)(2,1)} collective-permute-done((bf16[512,2048]{1,0:T(8,128)(2,1)}, bf16[512,2048]{1,0:T(8,128)(2,1)}, u32[]{:S(2)}, u32[]{:S(2)}) %collective-permute-start.3) | collective-permute-done | bytes 2097184 | tf_op jit(solution)/shard_map/ppermute | solution.py:10
  160.8 7.2 %collective-permute-done = bf16[512]{0:T(512)(128)(2,1)S(1)} collective-permute-done((bf16[512]{0:T(512)(128)(2,1)S(1)}, bf16[512]{0:T(512)(128)(2,1)S(1)}, u32[]{:S(2)}, u32[]{:S(2)}) %collective-permute-start) | collective-permute-done | bytes 1056 | tf_op jit(solution)/shard_map/ppermute | solution.py:10
  168.1 4.7 %multiply_convert_fusion = (bf16[2,512,384]{2,1,0:T(8,128)(2,1)}, bf16[1,2,512,384]{3,2,1,0:T(8,128)(2,1)}, bf16[2,512,384]{2,1,0:T(8,128)(2,1)}) fusion(f32[2,512,384]{2,1,0:T(8,128)} %reduce-scatter.8.cloned.1.call-done, f32[2,512]{1,0:T(2,128)S(1)} %pad_maximum_fusion.4, f32[2,512,384]{2,1,0:T(8,128)} %reduce-scatter.4.cloned.1.call-done, ...), kind=kLoop, calls=%fused_computation.65 | loop fusion | flops 6684672 | bytes 7081984 | tf_op jit(solution)/shard_map/convert_element_type | solution.py:37
  174.4 5.0 %all_to_all.5 = bf16[2,2,512,384]{3,2,1,0:T(8,128)(2,1)S(1)} all-to-all(bf16[2,2,512,384]{3,2,1,0:T(8,128)(2,1)S(1)} %pad_maximum_fusion.3), channel_id=1, replica_groups=mesh['expert'=16,'dp'=2] {'dp'}, dimensions={0} | all-to-all | bytes 3145728 | tf_op jit(solution)/shard_map/all_to_all | solution.py:116
  185.4 5.4 %convolution_convert_fusion.5 = bf16[768,2048]{1,0:T(8,128)(2,1)} fusion(bf16[512,768]{0,1:T(8,128)(2,1)} %bitcast.108, bf16[512,2048]{1,0:T(8,128)(2,1)} %gather_fusion.2, pred[512]{0:T(512)(128)(4,1)S(1)} %get-tuple-element.12), kind=kOutput, calls=%fused_computation.25 | convolution fusion | flops 1613234176 | bytes 6029824 | tf_op jit(solution)/shard_map/dot_general | solution.py:51
  190.9 3.8 %fusion.27 = f32[512,2048]{1,0:T(8,128)} fusion(bf16[512,768]{0,1:T(8,128)(2,1)S(1)} %bitcast.109, bf16[1,768,2048]{2,1,0:T(8,128)(2,1)S(1)} %copy-done), kind=kOutput, calls=%fused_computation.50 | convolution fusion | flops 1610612736 | bytes 8126464 | tf_op jit(solution)/shard_map/dot_general | solution.py:47
  194.7 3.8 %convolution_convert_fusion.4 = bf16[768,2048]{1,0:T(8,128)(2,1)S(1)} fusion(bf16[512,768]{0,1:T(8,128)(2,1)} %bitcast.110, bf16[512,2048]{1,0:T(8,128)(2,1)} %collective-permute-done.1), kind=kOutput, calls=%fused_computation.24 | convolution fusion | flops 1612185600 | bytes 6029312 | tf_op jit(solution)/shard_map/dot_general | solution.py:51
  201.6 5.7 %convolution_convert_fusion.2 = bf16[768,2048]{1,0:T(8,128)(2,1)} fusion(bf16[512,2048]{1,0:T(8,128)(2,1)} %collective-permute-done.1, bf16[2,512,768]{2,1,0:T(8,128)(2,1)} %all-gather.5.cloned.1.call-done), kind=kOutput, calls=%fused_computation.22 | convolution fusion | flops 1612185600 | bytes 6029312 | tf_op jit(solution)/shard_map/dot_general | solution.py:52
  207.3 3.6 %convolution_convert_fusion.3 = bf16[768,2048]{1,0:T(8,128)(2,1)} fusion(bf16[2,512,768]{2,1,0:T(8,128)(2,1)S(1)} %copy-done.12, bf16[512,2048]{1,0:T(8,128)(2,1)S(1)} %copy-done.5, pred[512]{0:T(512)(128)(4,1)S(1)} %get-tuple-element.12), kind=kOutput, calls=%fused_computation.23 | convolution fusion | flops 1613234176 | bytes 6029824 | tf_op jit(solution)/shard_map/dot_general | solution.py:52
  210.9 5.5 %convolution_convert_fusion = bf16[768,2048]{1,0:T(8,128)(2,1)} fusion(bf16[512,2048]{1,0:T(8,128)(2,1)} %collective-permute-done.3, bf16[2,512,768]{2,1,0:T(8,128)(2,1)} %all-gather.3.cloned.1.call-done), kind=kOutput, calls=%fused_computation.20 | convolution fusion | flops 1612185600 | bytes 6029312 | tf_op jit(solution)/shard_map/dot_general | solution.py:53
  216.4 3.8 %convolution_convert_fusion.1 = bf16[768,2048]{1,0:T(8,128)(2,1)} fusion(bf16[512,2048]{1,0:T(8,128)(2,1)S(1)} %copy-done.6, pred[512]{0:T(512)(128)(4,1)S(1)} %get-tuple-element.12, bf16[2,512,768]{2,1,0:T(8,128)(2,1)S(1)} %copy-done.14), kind=kOutput, calls=%fused_computation.21 | convolution fusion | flops 1613234176 | bytes 6029824 | tf_op jit(solution)/shard_map/dot_general | solution.py:53
  225.3 5.2 %collective-permute-start.4 = (bf16[512,2048]{1,0:T(8,128)(2,1)}, bf16[512,2048]{1,0:T(8,128)(2,1)}, u32[]{:S(2)}, u32[]{:S(2)}) collective-permute-start(bf16[512,2048]{1,0:T(8,128)(2,1)} %add_convert_fusion.3), channel_id=1, source_target_pairs={{0,30},{2,0},{4,2},{6,4},{8,6},{10,8},{12,10},{14,12},{16,14},{18,... | collective-permute-start | bytes 6291464 | tf_op jit(solution)/shard_map/ppermute | solution.py:10
  234.2 3.8 %fusion.15 = f32[512,2048]{1,0:T(8,128)} fusion(bf16[1,768,2048]{2,1,0:T(8,128)(2,1)S(1)} %copy-done.9, bf16[2,512,768]{2,1,0:T(8,128)(2,1)S(1)} %copy-done.14), kind=kOutput, calls=%fused_computation.38 | convolution fusion | flops 1610612736 | bytes 8126464 | tf_op jit(solution)/shard_map/dot_general | solution.py:46
  237.9 11.0 %scatter_custom_fusion = f32[512,2048]{1,0:T(8,128)} fusion(s32[512]{0:T(512)S(1)} %bitcast.118, f32[512,2048]{1,0:T(8,128)} %fusion.15, f32[]{:T(128)} %constant.31.clone.1), kind=kCustom, calls=%fused_computation.58 | custom fusion | flops 1048576 | bytes 4194816 | tf_op jit(solution)/shard_map/scatter-add | solution.py:155
  249.0 5.9 %fusion.19 = f32[512,2048]{1,0:T(8,128)} fusion(bf16[1,768,2048]{2,1,0:T(8,128)(2,1)} %param.20, bf16[2,512,768]{2,1,0:T(8,128)(2,1)} %all-gather.5.cloned.1.call-done), kind=kOutput, calls=%fused_computation.42 | convolution fusion | flops 1610612736 | bytes 8126464 | tf_op jit(solution)/shard_map/dot_general | solution.py:48
  254.9 12.5 %scatter_custom_fusion.2 = f32[512,2048]{1,0:T(8,128)} fusion(s32[512]{0:T(512)S(1)} %bitcast.119, f32[512,2048]{1,0:T(8,128)} %fusion.27, f32[512,2048]{1,0:T(8,128)} %fusion.19, f32[]{:T(128)} %constant.31.clone.1), kind=kCustom, calls=%fused_computation.16 | custom fusion | flops 2097152 | bytes 12582916 | tf_op jit(solution)/shard_map/scatter-add | solution.py:157
  267.4 6.2 %fusion.7 = bf16[1,768,2048]{2,1,0:T(8,128)(2,1)} fusion(bf16[768,2048]{1,0:T(8,128)(2,1)} %convolution_convert_fusion.2, bf16[768,2048]{1,0:T(8,128)(2,1)} %convolution_convert_fusion.3), kind=kLoop, calls=%fused_computation.27 | loop fusion | flops 6291456 | bytes 9437184 | tf_op jit(solution)/shard_map/broadcast_in_dim | solution.py:162
  276.8 12.4 %scatter_custom_fusion.3 = f32[512,2048]{1,0:T(8,128)} fusion(f32[512,2048]{1,0:T(8,128)} %scatter_custom_fusion.2, s32[512]{0:T(512)S(1)} %bitcast.116, bf16[512,2048]{1,0:T(8,128)(2,1)} %collective-permute-done.4), kind=kCustom, calls=%fused_computation.13 | custom fusion | flops 2097152 | bytes 6291456 | tf_op jit(solution)/shard_map/scatter-add | solution.py:157
  289.3 3.8 %convert_element_type.116 = bf16[512,2048]{1,0:T(8,128)(2,1)} convert(f32[512,2048]{1,0:T(8,128)} %scatter_custom_fusion.3) | non-fusion elementwise | flops 1048576 | bytes 6291456 | tf_op jit(solution)/shard_map/convert_element_type | solution.py:160
  293.1 27.8 %collective-permute-done.2 = bf16[512,2048]{1,0:T(8,128)(2,1)} collective-permute-done((bf16[512,2048]{1,0:T(8,128)(2,1)}, bf16[512,2048]{1,0:T(8,128)(2,1)}, u32[]{:S(2)}, u32[]{:S(2)}) %collective-permute-start.2) | collective-permute-done | bytes 2097184 | tf_op jit(solution)/shard_map/ppermute | solution.py:10
  320.9 12.2 %scatter_custom_fusion.1 = f32[512,2048]{1,0:T(8,128)} fusion(f32[512,2048]{1,0:T(8,128)} %scatter_custom_fusion, s32[512]{0:T(512)S(1)} %bitcast.117, bf16[512,2048]{1,0:T(8,128)(2,1)} %collective-permute-done.2), kind=kCustom, calls=%fused_computation.18 | custom fusion | flops 2097152 | bytes 6291456 | tf_op jit(solution)/shard_map/scatter-add | solution.py:155
  333.2 3.8 %convert_element_type.111 = bf16[512,2048]{1,0:T(8,128)(2,1)} convert(f32[512,2048]{1,0:T(8,128)} %scatter_custom_fusion.1) | non-fusion elementwise | flops 1048576 | bytes 6291456 | tf_op jit(solution)/shard_map/convert_element_type | solution.py:159
  (100 shorter events, 52.7 us)
Async XLA Ops:
  7.2 43.3 %copy-start = (bf16[1,768,2048]{2,1,0:T(8,128)(2,1)S(1)}, bf16[1,768,2048]{2,1,0:T(8,128)(2,1)}, u32[]{:S(2)}) copy-start(bf16[1,768,2048]{2,1,0:T(8,128)(2,1)} %param.19) | copy-start | bytes 9437188
  7.2 160.8 %reduce-scatter.4.cloned.1.call-start = ((), (), s32[]{:S(2)}) async-start(), calls=%async_computation.4 | async-start | bytes 4718592 | tf_op jit(solution)/shard_map/reduce_scatter | solution.py:107
  19.0 7.1 %copy-start.15 = (s32[16]{0:T(128)S(1)}, s32[16]{0:T(128)}, u32[]{:S(2)}) copy-start(s32[16]{0:T(128)} %param.18) | copy-start | bytes 196
  35.5 53.2 %collective-permute-start.1 = (bf16[512,2048]{1,0:T(8,128)(2,1)}, bf16[512,2048]{1,0:T(8,128)(2,1)}, u32[]{:S(2)}, u32[]{:S(2)}) collective-permute-start(bf16[512,2048]{1,0:T(8,128)(2,1)} %get-tuple-element.27), channel_id=1, source_target_pairs={{0,2},{2,4},{4,6},{6,8},{8,10},{10,12},{12,14},{14,16},{16,18},{18... | collective-permute-start | bytes 6291464 | tf_op jit(solution)/shard_map/ppermute | solution.py:10
  94.0 74.1 %reduce-scatter.6.cloned.1.call-start = ((), (), s32[]{:S(2)}) async-start(), calls=%async_computation.5 | async-start | bytes 4718592 | tf_op jit(solution)/shard_map/reduce_scatter | solution.py:108
  94.0 4.5 %copy-start.10 = (bf16[1,768,2048]{2,1,0:T(8,128)(2,1)S(1)}, bf16[1,768,2048]{2,1,0:T(8,128)(2,1)}, u32[]{:S(2)}) copy-start(bf16[1,768,2048]{2,1,0:T(8,128)(2,1)} %param.20) | copy-start | bytes 9437188
  103.9 64.2 %reduce-scatter.8.cloned.1.call-start = ((), (), s32[]{:S(2)}) async-start(), calls=%async_computation.7 | async-start | bytes 4718592 | tf_op jit(solution)/shard_map/reduce_scatter | solution.py:109
  103.9 51.4 %collective-permute-start.3 = (bf16[512,2048]{1,0:T(8,128)(2,1)}, bf16[512,2048]{1,0:T(8,128)(2,1)}, u32[]{:S(2)}, u32[]{:S(2)}) collective-permute-start(bf16[512,2048]{1,0:T(8,128)(2,1)} %get-tuple-element.26), channel_id=1, source_target_pairs={{0,2},{2,4},{4,6},{6,8},{8,10},{10,12},{12,14},{14,16},{16,18},{18... | collective-permute-start | bytes 6291464 | tf_op jit(solution)/shard_map/ppermute | solution.py:10
  111.6 43.7 %copy-start.8 = (bf16[1,768,2048]{2,1,0:T(8,128)(2,1)S(1)}, bf16[1,768,2048]{2,1,0:T(8,128)(2,1)}, u32[]{:S(2)}) copy-start(bf16[1,768,2048]{2,1,0:T(8,128)(2,1)} %param.21) | copy-start | bytes 9437188
  160.7 40.9 %all-gather.5.cloned.1.call-start = ((), (), s32[]{:S(2)}) async-start(), calls=%async_computation.8 | async-start | bytes 2359296 | tf_op jit(solution)/shard_map/all_gather | solution.py:118
  160.7 7.2 %collective-permute-start = (bf16[512]{0:T(512)(128)(2,1)S(1)}, bf16[512]{0:T(512)(128)(2,1)S(1)}, u32[]{:S(2)}, u32[]{:S(2)}) collective-permute-start(bf16[512]{0:T(512)(128)(2,1)S(1)} %get-tuple-element.13), channel_id=1, source_target_pairs={{0,2},{2,4},{4,6},{6,8},{8,10},{10,12},{12,14},{14,16},{16,18},{18... | collective-permute-start | bytes 3080 | tf_op jit(solution)/shard_map/ppermute | solution.py:10
  172.8 38.1 %all-gather.3.cloned.1.call-start = ((), (), s32[]{:S(2)}) async-start(), calls=%async_computation.6 | async-start | bytes 2359296 | tf_op jit(solution)/shard_map/all_gather | solution.py:114
  185.4 5.4 %copy-start.1 = (bf16[1,512,2,384]{1,3,2,0:T(8,128)(2,1)S(1)}, bf16[1,512,2,384]{1,3,2,0:T(8,128)(2,1)}, u32[]{:S(2)}) copy-start(bf16[1,512,2,384]{1,3,2,0:T(8,128)(2,1)} %copy.16) | copy-start | bytes 2359300
  194.7 3.8 %copy-start.4 = (bf16[768,2048]{1,0:T(8,128)(2,1)S(1)}, bf16[768,2048]{1,0:T(8,128)(2,1)}, u32[]{:S(2)}) copy-start(bf16[768,2048]{1,0:T(8,128)(2,1)} %convolution_convert_fusion.5) | copy-start | bytes 9437188
  201.6 5.7 %copy-start.5 = (bf16[512,2048]{1,0:T(8,128)(2,1)S(1)}, bf16[512,2048]{1,0:T(8,128)(2,1)}, u32[]{:S(2)}) copy-start(bf16[512,2048]{1,0:T(8,128)(2,1)} %gather_fusion.2) | copy-start | bytes 6291460
  201.6 5.7 %copy-start.12 = (bf16[2,512,768]{2,1,0:T(8,128)(2,1)S(1)}, bf16[2,512,768]{2,1,0:T(8,128)(2,1)}, u32[]{:S(2)}) copy-start(bf16[2,512,768]{2,1,0:T(8,128)(2,1)} %all-gather.5.cloned.1.call-done) | copy-start | bytes 4718596
  210.9 5.5 %copy-start.6 = (bf16[512,2048]{1,0:T(8,128)(2,1)S(1)}, bf16[512,2048]{1,0:T(8,128)(2,1)}, u32[]{:S(2)}) copy-start(bf16[512,2048]{1,0:T(8,128)(2,1)} %gather_fusion.4) | copy-start | bytes 6291460
  210.9 5.5 %copy-start.14 = (bf16[2,512,768]{2,1,0:T(8,128)(2,1)S(1)}, bf16[2,512,768]{2,1,0:T(8,128)(2,1)}, u32[]{:S(2)}) copy-start(bf16[2,512,768]{2,1,0:T(8,128)(2,1)} %all-gather.3.cloned.1.call-done) | copy-start | bytes 4718596
  216.3 3.9 %copy-start.11 = (bf16[1,768,2048]{2,1,0:T(8,128)(2,1)S(1)}, bf16[1,768,2048]{2,1,0:T(8,128)(2,1)}, u32[]{:S(2)}) copy-start(bf16[1,768,2048]{2,1,0:T(8,128)(2,1)} %param.20) | copy-start | bytes 9437188
  216.4 3.9 %copy-start.13 = (bf16[2,512,768]{2,1,0:T(8,128)(2,1)S(1)}, bf16[2,512,768]{2,1,0:T(8,128)(2,1)}, u32[]{:S(2)}) copy-start(bf16[2,512,768]{2,1,0:T(8,128)(2,1)} %all-gather.5.cloned.1.call-done) | copy-start | bytes 4718596
  220.2 1.8 copy-start.7
  222.0 8.5 %copy-start.9 = (bf16[1,768,2048]{2,1,0:T(8,128)(2,1)S(1)}, bf16[1,768,2048]{2,1,0:T(8,128)(2,1)}, u32[]{:S(2)}) copy-start(bf16[1,768,2048]{2,1,0:T(8,128)(2,1)} %param.21) | copy-start | bytes 9437188
  225.3 51.5 %collective-permute-start.4 = (bf16[512,2048]{1,0:T(8,128)(2,1)}, bf16[512,2048]{1,0:T(8,128)(2,1)}, u32[]{:S(2)}, u32[]{:S(2)}) collective-permute-start(bf16[512,2048]{1,0:T(8,128)(2,1)} %add_convert_fusion.3), channel_id=1, source_target_pairs={{0,30},{2,0},{4,2},{6,4},{8,6},{10,8},{12,10},{14,12},{16,14},{18,... | collective-permute-start | bytes 6291464 | tf_op jit(solution)/shard_map/ppermute | solution.py:10
  233.6 87.3 %collective-permute-start.2 = (bf16[512,2048]{1,0:T(8,128)(2,1)}, bf16[512,2048]{1,0:T(8,128)(2,1)}, u32[]{:S(2)}, u32[]{:S(2)}) collective-permute-start(bf16[512,2048]{1,0:T(8,128)(2,1)} %fusion.33), channel_id=1, source_target_pairs={{0,30},{2,0},{4,2},{6,4},{8,6},{10,8},{12,10},{14,12},{16,14},{18,... | collective-permute-start | bytes 6291464 | tf_op jit(solution)/shard_map/ppermute | solution.py:10
  267.4 6.2 %copy-start.2 = (bf16[768,2048]{1,0:T(8,128)(2,1)S(1)}, bf16[768,2048]{1,0:T(8,128)(2,1)}, u32[]{:S(2)}) copy-start(bf16[768,2048]{1,0:T(8,128)(2,1)} %convolution_convert_fusion) | copy-start | bytes 9437188
  267.4 6.2 %copy-start.3 = (bf16[768,2048]{1,0:T(8,128)(2,1)S(1)}, bf16[768,2048]{1,0:T(8,128)(2,1)}, u32[]{:S(2)}) copy-start(bf16[768,2048]{1,0:T(8,128)(2,1)} %convolution_convert_fusion.1) | copy-start | bytes 9437188
Sparse Core Ops, SparseCore 0:
  94.1 8.4 reduce-scatter.3
  105.4 12.2 reduce-scatter.5
  160.8 6.8 reduce-scatter.7
  172.9 10.6 all-gather.4
  194.8 10.6 all-gather.2
